TPU v7x, 32 devices: a whole 2x2x4 slice. The times are simulated.
32 devices in a mesh: zero: 4 (over x, core), width: 8 (over z, y).
Axes of the slice: x: 2, y: 2, z: 4, core: 2. Of those that a mesh axis runs over, the one named last changes fastest.
Arguments:
- weight_query: float32 [8192, 8192], P('zero', 'width'), may hold values from -0.09375 to 0.09375
- smooth_query: float32 [8192, 8192], P('zero', 'width'), may hold values from -0.0625 to 0.0625
- weight_key: float32 [8192, 512], P('zero', 'width'), may hold values from -0.09375 to 0.09375
- smooth_key: float32 [8192, 512], P('zero', 'width'), may hold values from -0.0625 to 0.0625
- weight_value: float32 [8192, 512], P('zero', 'width'), may hold values from -0.09375 to 0.09375
- smooth_value: float32 [8192, 512], P('zero', 'width'), may hold values from -0.0625 to 0.0625
- norm_train: float32 [8192], P(('zero', 'width')), may hold values from 0.25 to 1.75
- norm_step: float32 [8192], P(('zero', 'width')), may hold values from -0.3 to 0.3
Outputs:
- final_query: bfloat16 [8192, 8192], P(None, 'width')
- final_key: bfloat16 [8192, 512], P(None, 'width')
- final_value: bfloat16 [8192, 512], P(None, 'width')
- factor_query: float32 [8192], P('width')
- factor_key: float32 [512], P('width')
- factor_value: float32 [512], P('width')
- serve_norm: bfloat16 [8192], replicated
- result_query: float32 [8192, 8192], P('zero', 'width')
- result_key: float32 [8192, 512], P('zero', 'width')
- result_value: float32 [8192, 512], P('zero', 'width')
All inputs are finite; a program needn't handle non-finite values. Where the computation divides by a largest or mean magnitude, that divisor is 1e-20 or more.
Results may differ from a plain program's by a relative error of at most 0.001.
Values may be sent and summed in bfloat16 or wider, within the bound.
A program may use at most 128 MiB of HBM per device.

v0:
```python
import jax
import jax.numpy as jnp
from jax import lax
from jax.sharding import PartitionSpec as P

D_MODEL = 8192


keep_rate = 0.7


def on_device(
    weight_query,
    smooth_query,
    weight_key,
    smooth_key,
    weight_value,
    smooth_value,
    norm_train,
    norm_step,
):
    result_query = keep_rate * smooth_query + (1.0 - keep_rate) * weight_query
    result_key = keep_rate * smooth_key + (1.0 - keep_rate) * weight_key
    result_value = keep_rate * smooth_value + (1.0 - keep_rate) * weight_value
    total_query, total_key, total_value = lax.psum(
        (
            jnp.sum(jnp.abs(result_query), axis=0),
            jnp.sum(jnp.abs(result_key), axis=0),
            jnp.sum(jnp.abs(result_value), axis=0),
        ),
        "zero",
    )
    factor_query = total_query / D_MODEL
    factor_key = total_key / D_MODEL
    factor_value = total_value / D_MODEL
    narrow_query, narrow_key, narrow_value = (
        (result_query / factor_query).astype(jnp.bfloat16),
        (result_key / factor_key).astype(jnp.bfloat16),
        (result_value / factor_value).astype(jnp.bfloat16),
    )
    final_query, final_key, final_value = (
        lax.all_gather(narrow_query, "zero", axis=0, tiled=True),
        lax.all_gather(narrow_key, "zero", axis=0, tiled=True),
        lax.all_gather(narrow_value, "zero", axis=0, tiled=True),
    )
    serve_norm = lax.all_gather(
        (norm_train + norm_step).astype(jnp.bfloat16), ("zero", "width"), axis=0, tiled=True
    )
    return (
        final_query,
        final_key,
        final_value,
        factor_query,
        factor_key,
        factor_value,
        serve_norm,
        result_query,
        result_key,
        result_value,
    )


def solution(mesh):
    in_specs = (
        P("zero", "width"),
        P("zero", "width"),
        P("zero", "width"),
        P("zero", "width"),
        P("zero", "width"),
        P("zero", "width"),
        P(("zero", "width")),
        P(("zero", "width")),
    )
    out_specs = (
        P(None, "width"),
        P(None, "width"),
        P(None, "width"),
        P("width"),
        P("width"),
        P("width"),
        P(),
        P("zero", "width"),
        P("zero", "width"),
        P("zero", "width"),
    )
    return jax.shard_map(
        on_device, mesh=mesh, in_specs=in_specs, out_specs=out_specs, check_vma=False
    )
```

profile of v0, /device:TPU:0, one launch (start us, length us, event | category | flops | bytes accessed | tf_op | source)
XLA Modules:
  0.0 195.9 jit_solution(5785747271486764141)
XLA Ops:
  7.2 0.0 copy-start.4
  7.2 0.0 copy-start.5
  7.2 0.0 copy-start.6
  7.2 0.0 copy-start.7
  7.2 0.0 all-gather.7.cloned.1.call-start
  7.3 12.3 %abs_reduce_fusion = (f32[1024]{0:T(1024)S(1)}, f32[2048,1024]{1,0:T(8,128)}) fusion(f32[2048,1024]{1,0:T(8,128)} %param.8, f32[2048,1024]{1,0:T(8,128)} %param.9), kind=kLoop, calls=%fused_computation.1 | loop fusion | flops 10484736 | bytes 25169920 | tf_op jit(solution)/shard_map/reduce_sum | solution.py:27
  19.5 0.0 copy-done.4
  19.5 0.0 copy-done.5
  19.5 0.0 copy-done.6
  19.5 0.0 copy-done.7
  19.6 0.3 abs_reduce_fusion.1
  19.9 0.0 copy-start
  19.9 0.0 copy-start.1
  19.9 8.5 %all-reduce = (f32[1024]{0:T(1024)S(1)}, f32[64]{0:T(128)S(1)}, f32[64]{0:T(128)S(1)}) all-reduce(f32[1024]{0:T(1024)S(1)} %get-tuple-element.17, f32[64]{0:T(128)S(1)} %get-tuple-element.19, f32[64]{0:T(128)S(1)} %get-tuple-element.13), channel_id=1, replica_groups=mesh['zero'=4,'width'=8] {'zero'}, use_global_device_ids=true, to_apply=%region_1.0 | all-reduce | flops 1152 | bytes 9216 | tf_op jit(solution)/shard_map/psum | solution.py:25
  28.4 0.0 copy-start.11
  28.4 0.8 divide_convert_fusion.2
  29.2 0.0 all-gather.7.cloned.1.call-update
  29.3 0.0 all-gather.9.cloned.1.call-start
  29.3 0.0 copy-start.12
  29.3 0.8 divide_convert_fusion.1
  30.1 0.0 all-gather.9.cloned.1.call-update
  30.2 0.0 all-gather.5.cloned.1.call-start
  30.2 0.0 copy-start.8
  30.2 0.0 copy-start.9
  30.2 0.0 copy-start.10
  30.3 6.7 %divide_convert_fusion = bf16[2048,1024]{1,0:T(8,128)(2,1)} fusion(f32[2048,1024]{1,0:T(8,128)} %get-tuple-element.38, f32[1024]{0:T(1024)S(1)} %broadcast_multiply_fusion), kind=kLoop, calls=%fused_computation | loop fusion | flops 4194304 | bytes 12587008 | tf_op jit(solution)/shard_map/convert_element_type | solution.py:37
  36.9 0.0 all-gather.5.cloned.1.call-update
  37.0 0.0 copy-done
  37.0 0.0 copy-done.1
  37.0 0.0 copy-done.11
  37.0 0.0 copy-done.12
  37.0 0.0 copy-done.8
  37.0 0.0 copy-done.9
  37.0 0.0 copy-done.10
  37.1 67.2 %all-gather = bf16[32,1,256]{2,1,0:T(2,128)(2,1)S(1)} all-gather(bf16[1,1,256]{2,1,0:T(2,128)(2,1)S(1)} %reshape.23), channel_id=1, replica_groups=mesh['zero'=4,'width'=8] {'zero','width'}, dimensions={0}, use_global_device_ids=true | all-gather | bytes 16896 | tf_op jit(solution)/shard_map/all_gather | solution.py:46
  104.2 0.1 reduce
  104.3 0.6 copy.18
  105.0 0.0 all-gather.7.cloned.1.call-done
  105.0 0.0 all-gather.9.cloned.1.call-done
  105.0 68.4 %all-gather.5.cloned.1.call-done = bf16[8192,1024]{1,0:T(8,128)(2,1)} async-done(((bf16[2048,1024]{1,0:T(8,128)(2,1)}), bf16[8192,1024]{1,0:T(8,128)(2,1)}) %all-gather.5.cloned.1.call-update) | async-done | bytes 16777232 | tf_op jit(solution)/shard_map/all_gather | solution.py:42
  173.4 0.0 copy-start.2
  173.4 0.0 copy-start.3
  173.4 14.1 %copy.22 = bf16[8192,1024]{1,0:T(8,128)(2,1)} copy(bf16[8192,1024]{1,0:T(8,128)(2,1)} %all-gather.5.cloned.1.call-done) | data formatting | bytes 33554432
  187.4 0.0 copy-done.2
  187.4 1.0 copy.23
  188.4 0.0 copy-done.3
  188.4 1.0 copy.24
  (5 shorter events, 0.0 us)
Async XLA Ops:
  7.2 12.4 %copy-start.4 = (f32[2048,64]{0,1:T(8,128)S(1)}, f32[2048,64]{0,1:T(8,128)}, u32[]{:S(2)}) copy-start(f32[2048,64]{0,1:T(8,128)} %param.12) | copy-start | bytes 1572868
  7.2 12.3 %copy-start.5 = (f32[2048,64]{0,1:T(8,128)S(1)}, f32[2048,64]{0,1:T(8,128)}, u32[]{:S(2)}) copy-start(f32[2048,64]{0,1:T(8,128)} %param.13) | copy-start | bytes 1572868
  7.2 12.3 %copy-start.6 = (f32[2048,64]{0,1:T(8,128)S(1)}, f32[2048,64]{0,1:T(8,128)}, u32[]{:S(2)}) copy-start(f32[2048,64]{0,1:T(8,128)} %param.10) | copy-start | bytes 1572868
  7.2 12.3 %copy-start.7 = (f32[2048,64]{0,1:T(8,128)S(1)}, f32[2048,64]{0,1:T(8,128)}, u32[]{:S(2)}) copy-start(f32[2048,64]{0,1:T(8,128)} %param.11) | copy-start | bytes 1572868
  7.2 97.7 %all-gather.7.cloned.1.call-start = ((), (), s32[]{:S(2)}) async-start(), calls=%async_computation.1 | async-start | bytes 1310720 | tf_op jit(solution)/shard_map/all_gather | solution.py:43
  19.9 17.1 %copy-start = (f32[2048,64]{0,1:T(8,128)}, f32[2048,64]{0,1:T(8,128)S(1)}, u32[]{:S(2)}) copy-start(f32[2048,64]{0,1:T(8,128)S(1)} %get-tuple-element.40) | copy-start | bytes 1572868
  19.9 17.1 %copy-start.1 = (f32[2048,64]{0,1:T(8,128)}, f32[2048,64]{0,1:T(8,128)S(1)}, u32[]{:S(2)}) copy-start(f32[2048,64]{0,1:T(8,128)S(1)} %get-tuple-element.39) | copy-start | bytes 1572868
  28.4 8.6 %copy-start.11 = (f32[64]{0:T(128)}, f32[64]{0:T(128)S(1)}, u32[]{:S(2)}) copy-start(f32[64]{0:T(128)S(1)} %broadcast_multiply_fusion.2) | copy-start | bytes 772
  29.3 75.7 %all-gather.9.cloned.1.call-start = ((), (), s32[]{:S(2)}) async-start(), calls=%async_computation.2 | async-start | bytes 1310720 | tf_op jit(solution)/shard_map/all_gather | solution.py:44
  29.3 7.7 %copy-start.12 = (f32[64]{0:T(128)}, f32[64]{0:T(128)S(1)}, u32[]{:S(2)}) copy-start(f32[64]{0:T(128)S(1)} %broadcast_multiply_fusion.1) | copy-start | bytes 772
  30.2 143.2 %all-gather.5.cloned.1.call-start = ((), (), s32[]{:S(2)}) async-start(), calls=%async_computation | async-start | bytes 20971520 | tf_op jit(solution)/shard_map/all_gather | solution.py:42
  30.2 6.8 %copy-start.8 = (f32[1024]{0:T(1024)}, f32[1024]{0:T(1024)S(1)}, u32[]{:S(2)}) copy-start(f32[1024]{0:T(1024)S(1)} %broadcast_multiply_fusion) | copy-start | bytes 12292
  30.2 6.8 %copy-start.9 = (f32[256]{0:T(256)S(1)}, f32[256]{0:T(256)}, u32[]{:S(2)}) copy-start(f32[256]{0:T(256)} %param.14) | copy-start | bytes 3076
  30.2 6.8 %copy-start.10 = (f32[256]{0:T(256)S(1)}, f32[256]{0:T(256)}, u32[]{:S(2)}) copy-start(f32[256]{0:T(256)} %param.15) | copy-start | bytes 3076
  173.4 14.1 %copy-start.2 = (bf16[8192,64]{0,1:T(8,128)(2,1)S(1)}, bf16[8192,64]{0,1:T(8,128)(2,1)}, u32[]{:S(2)}) copy-start(bf16[8192,64]{0,1:T(8,128)(2,1)} %all-gather.7.cloned.1.call-done) | copy-start | bytes 3145732
  173.4 15.0 %copy-start.3 = (bf16[8192,64]{0,1:T(8,128)(2,1)S(1)}, bf16[8192,64]{0,1:T(8,128)(2,1)}, u32[]{:S(2)}) copy-start(bf16[8192,64]{0,1:T(8,128)(2,1)} %all-gather.9.cloned.1.call-done) | copy-start | bytes 3145732
Sparse Core Ops, SparseCore 0:
  29.4 17.0 all-gather.6
  48.6 16.6 all-gather.8
  67.4 105.8 all-gather.4
where the time goes:
time: 196 us
  blocking collectives  75.7 us (39%)
  waiting for transfers between devices  68.5 us (35%)
  other arithmetic  21 us (11%)
  local copies, waits for them, and re-layouts  16.7 us (9%)
  between operations  14 us (7%)
    all_gather x1, waiting for transfers between devices, on_device(): lax.all_gather(narrow_query, 'zero', axis=0, tiled=True)  68.4 us
    all_gather x1, blocking collectives, on_device(): lax.all_gather((norm_train + norm_step).astype(jnp.bfloat16), ('zero', 'w...  67.2 us
    unnamed x31, local copies, waits for them, and re-layouts  16.7 us
    reduce_sum x1, other arithmetic, on_device(): jnp.sum(jnp.abs(result_query), axis=0)  12.3 us
    psum x1, blocking collectives, on_device(): lax.psum((jnp.sum(jnp.abs(result_query), axis=0), jnp.sum(jnp.abs(result_...  8.51 us
    convert_element_type x1, other arithmetic, on_device(): (result_query / factor_query).astype(jnp.bfloat16)  6.68 us
  transfers between devices with their start and end apart: 3, of which 1 were waited for; matrix products, arithmetic and copies ran while one was open for 4% of the time, Pallas kernels for 0%

commit v1 on v0

v1 whole, which is shorter than its diff:
```python
import functools

import jax
import jax.numpy as jnp
from jax import lax
from jax.experimental import pallas as pl
from jax.experimental.pallas import tpu as pltpu
from jax.sharding import PartitionSpec as P

keep_rate = 0.7
CORES = 2
STEP = 16
PARTS = (0.35, 0.30, 0.20, 0.11, 0.04)
MESH = pl.DeviceIdType.MESH


def blend(smooth, weight):
    return keep_rate * smooth + (1.0 - keep_rate) * weight


def heights_of(rows):
    cuts = [0]
    done = 0.0
    for part in PARTS[:-1]:
        done += part
        cuts.append(int(rows * done) // 64 * 64)
    cuts.append(rows)
    return [b - a for a, b in zip(cuts, cuts[1:])]


def head_kernel(zeros, heights, blocks, *refs):
    wq, sq, wk, sk, wv, sv = refs[:6]
    count = len(heights)
    narrow_out = refs[6 : 6 + count]
    kv_out, factor = refs[6 + count : 8 + count]
    (vwq, vsq, vw, vs, narrow, narrow_kv, sums, got,
     in_sem, small_sem, out_sem, send_sem, recv_sem) = refs[8 + count :]
    rows, wide = wq.shape
    small = wk.shape[0]
    both = 2 * small
    block = rows // blocks
    me = lax.axis_index("zero")

    smalls = [
        pltpu.make_async_copy(src, dst, small_sem.at[i])
        for i, (src, dst) in enumerate((
            (wk, vw.at[pl.ds(0, small)]), (sk, vs.at[pl.ds(0, small)]),
            (wv, vw.at[pl.ds(small, small)]), (sv, vs.at[pl.ds(small, small)]),
        ))
    ]
    for copy in smalls:
        copy.start()
    copies = []
    for b in range(blocks):
        at = pl.ds(b * block, block)
        pair = (
            pltpu.make_async_copy(wq.at[at], vwq.at[at], in_sem.at[0, b]),
            pltpu.make_async_copy(sq.at[at], vsq.at[at], in_sem.at[1, b]),
        )
        for copy in pair:
            copy.start()
        copies.append(pair)
    barrier = pltpu.get_barrier_semaphore()
    for k in range(1, zeros):
        pl.semaphore_signal(
            barrier, inc=1, device_id={"zero": lax.rem(me + k, zeros)}, device_id_type=MESH
        )

    for copy in smalls:
        copy.wait()

    def add_small(i, acc):
        at = pl.ds(pl.multiple_of(i * 128, 128), 128)
        value = blend(vs[:, at], vw[:, at])
        vw[:, at] = value
        return acc + jnp.abs(value)

    total_kv = lax.fori_loop(0, rows // 128, add_small, jnp.zeros((both, 128), jnp.float32))
    sums[:, wide : wide + both] = jnp.sum(total_kv.T, axis=0, keepdims=True)

    total_q = jnp.zeros((8, wide), jnp.float32)
    for b in range(blocks):
        for copy in copies[b]:
            copy.wait()

        def add(i, acc, b=b):
            at = pl.ds(pl.multiple_of(b * block + i * STEP, STEP), STEP)
            value = blend(vsq[at, :], vwq[at, :])
            vwq[at, :] = value
            size = jnp.abs(value)
            for r in range(0, STEP, 8):
                acc = acc + size[r : r + 8]
            return acc

        total_q = lax.fori_loop(0, block // STEP, add, total_q)
    sums[:, 0:wide] = jnp.sum(total_q, axis=0, keepdims=True)

    pl.semaphore_wait(barrier, zeros - 1)
    sends = []
    for k in range(1, zeros):
        send = pltpu.make_async_remote_copy(
            src_ref=sums, dst_ref=got.at[k - 1],
            send_sem=send_sem.at[k - 1], recv_sem=recv_sem.at[k - 1],
            device_id={"zero": lax.rem(me + k, zeros)}, device_id_type=MESH,
        )
        send.start()
        sends.append(send)
    for send in sends:
        send.wait()
    total = sums[...]
    for k in range(zeros - 1):
        total = total + got[k]
    scale = total / (rows * zeros)
    factor[...] = scale
    back = 1.0 / scale
    back_q = back[:, 0:wide]
    back_kv = jnp.broadcast_to(back[:, wide : wide + both], (128, both)).T

    def scale_small(i, carry):
        at = pl.ds(pl.multiple_of(i * 128, 128), 128)
        narrow_kv[:, at] = (vw[:, at] * back_kv).astype(jnp.bfloat16)
        return carry

    outs = []
    first = 0
    for n, height in enumerate(heights):

        def scale_rows(i, carry, first=first):
            at = pl.ds(pl.multiple_of(first + i * STEP, STEP), STEP)
            narrow[at, :] = (vwq[at, :] * back_q).astype(jnp.bfloat16)
            return carry

        lax.fori_loop(0, height // STEP, scale_rows, 0)
        out = pltpu.make_async_copy(
            narrow.at[pl.ds(first, height)], narrow_out[n], out_sem.at[n]
        )
        out.start()
        outs.append(out)
        first += height
    lax.fori_loop(0, rows // 128, scale_small, 0)
    out = pltpu.make_async_copy(narrow_kv, kv_out, out_sem.at[count])
    out.start()
    outs.append(out)
    for out in outs:
        out.wait()


def head(zeros, heights, wq, sq, wk, sk, wv, sv):
    rows, wide = wq.shape
    both = 2 * wk.shape[0]
    blocks = 8
    f32, bf16 = jnp.float32, jnp.bfloat16
    return pl.pallas_call(
        functools.partial(head_kernel, zeros, heights, blocks),
        out_shape=[jax.ShapeDtypeStruct((h, wide), bf16) for h in heights]
        + [jax.ShapeDtypeStruct((both, rows), bf16), jax.ShapeDtypeStruct((1, wide + both), f32)],
        in_specs=[pl.BlockSpec(memory_space=pl.ANY)] * 6,
        out_specs=[pl.BlockSpec(memory_space=pl.ANY)] * (len(heights) + 1)
        + [pl.BlockSpec(memory_space=pltpu.VMEM)],
        scratch_shapes=[
            pltpu.VMEM((rows, wide), f32), pltpu.VMEM((rows, wide), f32),
            pltpu.VMEM((both, rows), f32), pltpu.VMEM((both, rows), f32),
            pltpu.VMEM((rows, wide), bf16), pltpu.VMEM((both, rows), bf16),
            pltpu.VMEM((1, wide + both), f32), pltpu.VMEM((zeros - 1, 1, wide + both), f32),
            pltpu.SemaphoreType.DMA((2, blocks)),
            pltpu.SemaphoreType.DMA((4,)),
            pltpu.SemaphoreType.DMA((len(heights) + 1,)),
            pltpu.SemaphoreType.DMA((zeros - 1,)),
            pltpu.SemaphoreType.DMA((zeros - 1,)),
        ],
        compiler_params=pltpu.CompilerParams(
            collective_id=0, has_side_effects=True, vmem_limit_bytes=60 * 2**20
        ),
        cost_estimate=pl.CostEstimate(
            flops=6 * rows * wide, bytes_accessed=12 * rows * wide, transcendentals=0
        ),
    )(wq, sq, wk, sk, wv, sv)


def norm_kernel(zeros, widths, train, step, out, mine, all_of, send_sem, recv_sem):
    count = zeros * widths
    me_zero, me_width = lax.axis_index("zero"), lax.axis_index("width")
    me = me_zero * widths + me_width
    barrier = pltpu.get_barrier_semaphore()

    def place(k):
        other = lax.rem(me + k, count)
        return {"zero": other // widths, "width": lax.rem(other, widths)}

    def greet(k, carry):
        pl.semaphore_signal(barrier, inc=1, device_id=place(k), device_id_type=MESH)
        return carry

    lax.fori_loop(1, count, greet, 0)
    mine[...] = train[...] + step[...]
    pl.semaphore_wait(barrier, count - 1)

    def copy(k):
        return pltpu.make_async_remote_copy(
            src_ref=mine, dst_ref=all_of.at[k],
            send_sem=send_sem.at[k], recv_sem=recv_sem.at[k],
            device_id=place(k), device_id_type=MESH,
        )

    def send(k, carry):
        copy(k).start()
        return carry

    lax.fori_loop(1, count, send, 0)
    out[me] = mine[...]

    def take(k, carry):
        copy(k).wait()
        out[lax.rem(me + count - k, count)] = all_of[k]
        return carry

    lax.fori_loop(1, count, take, 0)


def norm_gather(zeros, widths, train, step):
    count = zeros * widths
    size = train.shape[0]
    f32 = jnp.float32
    return pl.pallas_call(
        functools.partial(norm_kernel, zeros, widths),
        out_shape=jax.ShapeDtypeStruct((count, 1, size), f32),
        in_specs=[pl.BlockSpec(memory_space=pltpu.VMEM)] * 2,
        out_specs=pl.BlockSpec(memory_space=pltpu.VMEM),
        scratch_shapes=[
            pltpu.VMEM((1, size), f32),
            pltpu.VMEM((count, 1, size), f32),
            pltpu.SemaphoreType.DMA((count,)),
            pltpu.SemaphoreType.DMA((count,)),
        ],
        compiler_params=pltpu.CompilerParams(collective_id=1, has_side_effects=True),
        cost_estimate=pl.CostEstimate(flops=0, bytes_accessed=2**23, transcendentals=0),
    )(train.reshape(1, size), step.reshape(1, size))


def place_kernel(chips, outs_of, old_count, *refs):
    count = chips * CORES
    pieces = refs[:count]
    outs = refs[count + old_count : -3]
    buf, in_sem, out_sem = refs[-3:]
    me = lax.axis_index("zero")
    chip, core = me // CORES, lax.rem(me, CORES)
    ins, sent = [], []
    for p in range(count):
        copy = pltpu.make_async_copy(pieces[p], buf.at[p], in_sem.at[p])
        copy.start()
        ins.append(copy)
    for p in range(count):
        back, swap = p // CORES, p % CORES
        owner = lax.rem(chip + chips - back, chips) * CORES + lax.rem(core + swap, CORES)
        ins[p].wait()
        for n, (src, dst) in enumerate(outs_of(buf.at[p], outs, owner)):
            copy = pltpu.make_async_copy(src, dst, out_sem.at[n, p])
            copy.start()
            sent.append(copy)
    for copy in sent:
        copy.wait()


def place(chips, outs_of, shapes, pieces, old):
    count = chips * CORES
    bf16 = jnp.bfloat16
    old = () if old is None else tuple(old)
    return pl.pallas_call(
        functools.partial(place_kernel, chips, outs_of, len(old)),
        out_shape=[jax.ShapeDtypeStruct(shape, bf16) for shape in shapes],
        in_specs=[pl.BlockSpec(memory_space=pl.ANY)] * (count + len(old)),
        out_specs=[pl.BlockSpec(memory_space=pl.ANY)] * len(shapes),
        input_output_aliases={count + n: n for n in range(len(old))},
        scratch_shapes=[
            pltpu.VMEM((count,) + pieces[0].shape, bf16),
            pltpu.SemaphoreType.DMA((count,)),
            pltpu.SemaphoreType.DMA((len(shapes), count)),
        ],
        compiler_params=pltpu.CompilerParams(
            vmem_limit_bytes=2 * count * pieces[0].size + 2**20
        ),
        cost_estimate=pl.CostEstimate(
            flops=0, bytes_accessed=4 * count * pieces[0].size, transcendentals=0
        ),
    )(*pieces, *old)


def on_device(zeros, widths, wq, sq, wk, sk, wv, sv, train, step):
    rows, wide = wq.shape
    small = wk.shape[1]
    chips = zeros // CORES
    heights = heights_of(rows)
    *narrow, narrow_kv, factor = head(zeros, heights, wq, sq, wk.T, sk.T, wv.T, sv.T)
    across = [
        [(x * CORES + c, (x + k) % chips * CORES + c) for x in range(chips) for c in range(CORES)]
        for k in range(chips)
    ]
    swap = [(x * CORES + c, x * CORES + (c + 1) % CORES) for x in range(chips) for c in range(CORES)]

    def arrive(block):
        got = [block]
        for k in range(1, chips):
            got.append(lax.ppermute(block, "zero", across[k]))
        return got

    def pieces_of(blocks):
        return [p for b in blocks for p in (b, lax.ppermute(b, "zero", swap))]

    kv_blocks = arrive(narrow_kv)
    arrived = [arrive(block) for block in narrow]
    result_q = blend(sq, wq)
    result_k, result_v = blend(sk, wk), blend(sv, wv)
    serve = norm_gather(zeros, widths, train, step)

    def columns_of(src, outs, owner):
        at = pl.ds(pl.multiple_of(owner * rows, 128), rows)
        return [(src.at[pl.ds(n * small, small)], outs[n].at[:, at]) for n in range(2)]

    kv_blocks, (result_q, result_k, result_v, serve) = lax.optimization_barrier(
        (kv_blocks, (result_q, result_k, result_v, serve))
    )
    final_kv = place(chips, columns_of, [(small, rows * zeros)] * 2, pieces_of(kv_blocks), None)
    arrived[0], final_kv = lax.optimization_barrier((arrived[0], final_kv))
    final = None
    first = 0
    for n, blocks in enumerate(arrived):
        if n:
            blocks, final = lax.optimization_barrier((blocks, final))
        height = blocks[0].shape[0]

        def rows_of(src, outs, owner, first=first, height=height):
            at = pl.ds(pl.multiple_of(owner * rows + first, 64), height)
            return [(src, outs[0].at[at])]

        final = place(chips, rows_of, [(rows * zeros, wide)], pieces_of(blocks), final)
        first += height
    factor = factor.reshape(-1)
    return (
        final[0],
        final_kv[0].T,
        final_kv[1].T,
        factor[:wide],
        factor[wide : wide + small],
        factor[wide + small :],
        serve.reshape(-1).astype(jnp.bfloat16),
        result_q,
        result_k,
        result_v,
    )


def solution(mesh):
    grid = P("zero", "width")
    in_specs = (grid,) * 6 + (P(("zero", "width")),) * 2
    out_specs = (
        (P(None, "width"),) * 3 + (P("width"),) * 3 + (P(),) + (grid,) * 3
    )
    zeros, widths = mesh.shape["zero"], mesh.shape["width"]

    def whole(*args):
        return on_device(zeros, widths, *args)

    return jax.shard_map(
        whole, mesh=mesh, in_specs=in_specs, out_specs=out_specs, check_vma=False
    )
```

time: 196 us -> 148 us (0.76)
  blocking collectives: 75.7 us -> 0 us
  Pallas kernels: 0 us -> 65.5 us
  local copies, waits for them, and re-layouts: 16.7 us -> 1.83 us
  between operations: 14 us -> 0.76 us
  waiting for transfers between devices: 68.5 us -> 57.8 us
  starting transfers between devices: 0.12 us -> 7.4 us
  other arithmetic: 21 us -> 15 us
    all_gather x3 -> x0, waiting for transfers between devices: 68.4 us -> none  [the longest x1 68.4 us: on_device(): lax.all_gather(narrow_query, 'zero', axis=0, tiled=True)]
    all_gather x1 -> x0, blocking collectives: 67.2 us -> none  [on_device(): lax.all_gather((norm_train + norm_step).astype(jnp.bfloat16), ('zero', 'w...]
    pallas_call x0 -> x8, Pallas kernels: none -> 65.5 us  [the longest x1 33.3 us: norm_gather(): pl.pallas_call(functools.partial(norm_kernel, zeros, widths), out_shape=j...]
    ppermute x0 -> x18, waiting for transfers between devices: none -> 57.8 us  [the longest x6 44.4 us: arrive(): got.append(lax.ppermute(block, 'zero', across[k]))]
    unnamed x31 -> x17, local copies, waits for them, and re-layouts: 16.7 us -> 0.65 us
    add x0 -> x2, other arithmetic: none -> 15 us  [blend(): return keep_rate * smooth + (1.0 - keep_rate) * weight]
    reduce_sum x2 -> x0, other arithmetic: 12.6 us -> none  [the longest x1 12.3 us: on_device(): jnp.sum(jnp.abs(result_query), axis=0)]
    psum x1 -> x0, blocking collectives: 8.51 us -> none  [on_device(): lax.psum((jnp.sum(jnp.abs(result_query), axis=0), jnp.sum(jnp.abs(result_...]
  transfers between devices with their start and end apart: 3 -> 18, of which waited for: 1 -> 15; matrix products, arithmetic and copies ran while one was open for 4% -> 11% of each run, Pallas kernels for 0% -> 32%
where the time goes in v1:
time: 148 us
  Pallas kernels  65.5 us (44%)
  waiting for transfers between devices  57.8 us (39%)
  other arithmetic  15 us (10%)
  starting transfers between devices  7.4 us (5%)
  local copies, waits for them, and re-layouts  1.83 us (1%)
    ppermute x6, waiting for transfers between devices, arrive(): got.append(lax.ppermute(block, 'zero', across[k]))  44.4 us
    pallas_call x1, Pallas kernels, norm_gather(): pl.pallas_call(functools.partial(norm_kernel, zeros, widths), out_shape=j...  33.3 us
    pallas_call x1, Pallas kernels, head(): pl.pallas_call(functools.partial(head_kernel, zeros, heights, blocks), ou...  17.1 us
    pallas_call x6, Pallas kernels, place(): pl.pallas_call(functools.partial(place_kernel, chips, outs_of, len(old)),...  15.1 us
    add x2, other arithmetic, blend(): return keep_rate * smooth + (1.0 - keep_rate) * weight  15 us
    ppermute x12, waiting for transfers between devices, pieces_of(): return [p for b in blocks for p in (b, lax.ppermute(b, 'zero', swap))]  13.3 us
    ppermute x6, starting transfers between devices, arrive(): got.append(lax.ppermute(block, 'zero', across[k]))  4.21 us
    ppermute x12, starting transfers between devices, pieces_of(): return [p for b in blocks for p in (b, lax.ppermute(b, 'zero', swap))]  3.19 us
  transfers between devices with their start and end apart: 18, of which 15 were waited for; matrix products, arithmetic and copies ran while one was open for 11% of the time, Pallas kernels for 32%

profile of v1, /device:TPU:0, one launch (start us, length us, event | category | flops | bytes accessed | tf_op | source)
XLA Modules:
  0.0 148.3 jit_solution(5512586221452374593)
XLA Ops:
  0.6 17.1 %shard_map.159 = (bf16[704,1024]{1,0:T(8,128)(2,1)}, bf16[576,1024]{1,0:T(8,128)(2,1)}, bf16[448,1024]{1,0:T(8,128)(2,1)}, bf16[192,1024]{1,0:T(8,128)(2,1)}, bf...) custom-call(f32[2048,1024]{1,0:T(8,128)} %refs_0_.1, f32[2048,1024]{1,0:T(8,128)} %refs_1_.1, ...), custom_call_target="tpu_custom_call" | custom-call | flops 12582912 | bytes 25165824 | tf_op jit(solution)/shard_map/pallas_call | solution.py:153
  17.7 0.1 collective-permute-start.5
  17.8 2.0 %collective-permute-start.4 = (bf16[704,1024]{1,0:T(8,128)(2,1)}, bf16[704,1024]{1,0:T(8,128)(2,1)S(1)}, u32[]{:S(2)}, u32[]{:S(2)}) collective-permute-start(bf16[704,1024]{1,0:T(8,128)(2,1)} %get-tuple-element.51.refs_0_), channel_id=1, source_target_pairs={{0,16},{8,24},{16,0},{24,8},{1,17},{9,25},{17,1},{25,9},{2,18},{10... | collective-permute-start | bytes 4325384 | tf_op jit(solution)/shard_map/ppermute | solution.py:303
  19.8 12.3 %multiply_add_fusion = f32[2048,1024]{1,0:T(8,128)} fusion(f32[2048,1024]{1,0:T(8,128)} %refs_0_.1, f32[2048,1024]{1,0:T(8,128)} %refs_1_.1), kind=kLoop, calls=%fused_computation | loop fusion | flops 6291456 | bytes 25165824 | tf_op jit(solution)/shard_map/add | solution.py:18
  32.1 33.3 %shard_map.160 = f32[32,1,256]{2,1,0:T(1,128)} custom-call(f32[1,256]{1,0:T(1,128)} %bitcast.22, f32[1,256]{1,0:T(1,128)} %bitcast.23), custom_call_target="tpu_custom_call" | custom-call | bytes 8388608 | tf_op jit(solution)/shard_map/pallas_call | solution.py:224
  65.4 2.7 %multiply_add_fusion.1 = (f32[2048,64]{0,1:T(8,128)}, f32[2048,64]{0,1:T(8,128)}) fusion(f32[2048,64]{0,1:T(8,128)} %param.12, f32[2048,64]{0,1:T(8,128)} %param.13, f32[2048,64]{0,1:T(8,128)} %param.10, f32[2048,64]{0,1:T(8,128)} %param.11), kind=kLoop, calls=%fused_computation.1 | loop fusion | flops 786432 | bytes 3145728 | tf_op jit(solution)/shard_map/add | solution.py:18
  68.1 0.1 collective-permute-start.6
  68.2 0.5 collective-permute-start.7
  68.7 1.4 collective-permute-done.6.refs_1_
  70.1 0.7 collective-permute-done.7.refs_3_
  70.8 2.4 %shard_map.161 = (bf16[64,8192]{1,0:T(8,128)(2,1)}, bf16[64,8192]{1,0:T(8,128)(2,1)}) custom-call(bf16[128,2048]{1,0:T(8,128)(2,1)S(1)} %copy-done.3, bf16[128,2048]{1,0:T(8,128)(2,1)S(1)} %collective-permute-done.6.refs_1_, bf16[128,2048]{1,0:T(8,128)(2,1)} %collective-permute-done.5.refs_2_, bf16[128,2048]{1,0:T(8,128)(2,1)S(1)} %collective-permute-done.7.refs_3_), custom_call_target="tpu_custom_call" | custom-call | bytes 4194304 | tf_op jit(solution)/shard_map/pallas_call | solution.py:268
  73.3 0.2 collective-permute-start.8
  73.5 0.4 collective-permute-start.9
  73.9 0.5 collective-permute-start.3
  74.4 2.2 %collective-permute-done.8.refs_1_ = bf16[704,1024]{1,0:T(8,128)(2,1)S(1)} collective-permute-done((bf16[704,1024]{1,0:T(8,128)(2,1)S(1)}, bf16[704,1024]{1,0:T(8,128)(2,1)S(1)}, u32[]{:S(2)}, u32[]{:S(2)}) %collective-permute-start.8) | collective-permute-done | bytes 1441824 | tf_op jit(solution)/shard_map/ppermute | solution.py:307
  76.6 2.1 %collective-permute-done.9.refs_3_ = bf16[704,1024]{1,0:T(8,128)(2,1)S(1)} collective-permute-done((bf16[704,1024]{1,0:T(8,128)(2,1)S(1)}, bf16[704,1024]{1,0:T(8,128)(2,1)S(1)}, u32[]{:S(2)}, u32[]{:S(2)}) %collective-permute-start.9) | collective-permute-done | bytes 1441824 | tf_op jit(solution)/shard_map/ppermute | solution.py:307
  78.6 3.6 %shard_map.162.refs_4_ = bf16[8192,1024]{1,0:T(8,128)(2,1)} custom-call(bf16[704,1024]{1,0:T(8,128)(2,1)S(1)} %copy-done, bf16[704,1024]{1,0:T(8,128)(2,1)S(1)} %collective-permute-done.8.refs_1_, bf16[704,1024]{1,0:T(8,128)(2,1)S(1)} %collective-permute-done.4.refs_2_, bf16[704,1024]{1,0:T(8,128)(2,1)S(1)} %collective-permute-done.9.refs_3_), custom_call_target="tpu_custom_call" | custom-call | bytes 11534336 | tf_op jit(solution)/shard_map/pallas_call | solution.py:268
  82.3 19.8 %collective-permute-done.3.refs_2_ = bf16[576,1024]{1,0:T(8,128)(2,1)S(1)} collective-permute-done((bf16[576,1024]{1,0:T(8,128)(2,1)}, bf16[576,1024]{1,0:T(8,128)(2,1)S(1)}, u32[]{:S(2)}, u32[]{:S(2)}) %collective-permute-start.3) | collective-permute-done | bytes 1179680 | tf_op jit(solution)/shard_map/ppermute | solution.py:303
  102.1 0.0 collective-permute-start.10
  102.1 0.5 collective-permute-start.11
  102.6 0.5 collective-permute-start.2
  103.1 1.8 %collective-permute-done.10.refs_1_ = bf16[576,1024]{1,0:T(8,128)(2,1)S(1)} collective-permute-done((bf16[576,1024]{1,0:T(8,128)(2,1)S(1)}, bf16[576,1024]{1,0:T(8,128)(2,1)S(1)}, u32[]{:S(2)}, u32[]{:S(2)}) %collective-permute-start.10) | collective-permute-done | bytes 1179680 | tf_op jit(solution)/shard_map/ppermute | solution.py:307
  104.9 1.7 %collective-permute-done.11.refs_3_ = bf16[576,1024]{1,0:T(8,128)(2,1)S(1)} collective-permute-done((bf16[576,1024]{1,0:T(8,128)(2,1)S(1)}, bf16[576,1024]{1,0:T(8,128)(2,1)S(1)}, u32[]{:S(2)}, u32[]{:S(2)}) %collective-permute-start.11) | collective-permute-done | bytes 1179680 | tf_op jit(solution)/shard_map/ppermute | solution.py:307
  106.6 3.2 %shard_map.163.refs_4_ = bf16[8192,1024]{1,0:T(8,128)(2,1)} custom-call(bf16[576,1024]{1,0:T(8,128)(2,1)S(1)} %copy-done.1, bf16[576,1024]{1,0:T(8,128)(2,1)S(1)} %collective-permute-done.10.refs_1_, bf16[576,1024]{1,0:T(8,128)(2,1)S(1)} %collective-permute-done.3.refs_2_, ...), custom_call_target="tpu_custom_call", output_to_operand_aliasing={{}: (4, {})} | custom-call | bytes 9437184 | tf_op jit(solution)/shard_map/pallas_call | solution.py:268
  109.8 15.1 %collective-permute-done.2.refs_2_ = bf16[448,1024]{1,0:T(8,128)(2,1)S(1)} collective-permute-done((bf16[448,1024]{1,0:T(8,128)(2,1)S(1)}, bf16[448,1024]{1,0:T(8,128)(2,1)S(1)}, u32[]{:S(2)}, u32[]{:S(2)}) %collective-permute-start.2) | collective-permute-done | bytes 917536 | tf_op jit(solution)/shard_map/ppermute | solution.py:303
  124.9 0.0 collective-permute-start.12
  124.9 0.5 collective-permute-start.13
  125.4 0.5 collective-permute-start.1
  126.0 1.4 collective-permute-done.12.refs_1_
  127.4 1.3 collective-permute-done.13.refs_3_
  128.7 2.8 %shard_map.164.refs_4_ = bf16[8192,1024]{1,0:T(8,128)(2,1)} custom-call(bf16[448,1024]{1,0:T(8,128)(2,1)S(1)} %copy-done.2, bf16[448,1024]{1,0:T(8,128)(2,1)S(1)} %collective-permute-done.12.refs_1_, bf16[448,1024]{1,0:T(8,128)(2,1)S(1)} %collective-permute-done.2.refs_2_, ...), custom_call_target="tpu_custom_call", output_to_operand_aliasing={{}: (4, {})} | custom-call | bytes 7340032 | tf_op jit(solution)/shard_map/pallas_call | solution.py:268
  131.5 5.0 %collective-permute-done.1.refs_2_ = bf16[192,1024]{1,0:T(8,128)(2,1)S(1)} collective-permute-done((bf16[192,1024]{1,0:T(8,128)(2,1)S(1)}, bf16[192,1024]{1,0:T(8,128)(2,1)S(1)}, u32[]{:S(2)}, u32[]{:S(2)}) %collective-permute-start.1) | collective-permute-done | bytes 393248 | tf_op jit(solution)/shard_map/ppermute | solution.py:303
  136.5 0.0 collective-permute-start.14
  136.5 0.5 collective-permute-start.15
  137.0 0.5 collective-permute-start
  137.6 0.6 slice.18
  138.2 0.1 collective-permute-done.14.refs_1_
  138.2 0.6 collective-permute-done.15.refs_3_
  138.8 1.9 %shard_map.165.refs_4_ = bf16[8192,1024]{1,0:T(8,128)(2,1)} custom-call(bf16[192,1024]{1,0:T(8,128)(2,1)S(1)} %copy-done.4, bf16[192,1024]{1,0:T(8,128)(2,1)S(1)} %collective-permute-done.14.refs_1_, bf16[192,1024]{1,0:T(8,128)(2,1)S(1)} %collective-permute-done.1.refs_2_, ...), custom_call_target="tpu_custom_call", output_to_operand_aliasing={{}: (4, {})} | custom-call | bytes 3145728 | tf_op jit(solution)/shard_map/pallas_call | solution.py:268
  140.8 4.5 %collective-permute-done.refs_2_ = bf16[128,1024]{1,0:T(8,128)(2,1)S(1)} collective-permute-done((bf16[128,1024]{1,0:T(8,128)(2,1)S(1)}, bf16[128,1024]{1,0:T(8,128)(2,1)S(1)}, u32[]{:S(2)}, u32[]{:S(2)}) %collective-permute-start) | collective-permute-done | bytes 262176 | tf_op jit(solution)/shard_map/ppermute | solution.py:303
  145.2 0.0 collective-permute-start.16
  145.3 0.5 collective-permute-start.17
  145.8 0.6 slice_bitcast_fusion
  146.3 0.1 convert_reduce_fusion
  146.4 0.6 copy.22
  147.1 0.0 collective-permute-done.16.refs_1_
  147.1 0.1 collective-permute-done.17.refs_3_
  147.2 1.1 shard_map.166
  (18 shorter events, 0.0 us)
Async XLA Ops:
  17.7 50.4 %collective-permute-start.5 = (bf16[128,2048]{1,0:T(8,128)(2,1)}, bf16[128,2048]{1,0:T(8,128)(2,1)}, u32[]{:S(2)}, u32[]{:S(2)}) collective-permute-start(bf16[128,2048]{1,0:T(8,128)(2,1)} %get-tuple-element.47.refs_0_), channel_id=1, source_target_pairs={{0,16},{8,24},{16,0},{24,8},{1,17},{9,25},{17,1},{25,9},{2,18},{10... | collective-permute-start | bytes 1572872 | tf_op jit(solution)/shard_map/ppermute | solution.py:303
  17.8 50.3 %copy-start.3 = (bf16[128,2048]{1,0:T(8,128)(2,1)S(1)}, bf16[128,2048]{1,0:T(8,128)(2,1)}, u32[]{:S(2)}) copy-start(bf16[128,2048]{1,0:T(8,128)(2,1)} %get-tuple-element.47.refs_0_) | copy-start | bytes 1572868
  17.8 55.5 %copy-start = (bf16[704,1024]{1,0:T(8,128)(2,1)S(1)}, bf16[704,1024]{1,0:T(8,128)(2,1)}, u32[]{:S(2)}) copy-start(bf16[704,1024]{1,0:T(8,128)(2,1)} %get-tuple-element.51.refs_0_) | copy-start | bytes 4325380
  17.8 55.5 %collective-permute-start.4 = (bf16[704,1024]{1,0:T(8,128)(2,1)}, bf16[704,1024]{1,0:T(8,128)(2,1)S(1)}, u32[]{:S(2)}, u32[]{:S(2)}) collective-permute-start(bf16[704,1024]{1,0:T(8,128)(2,1)} %get-tuple-element.51.refs_0_), channel_id=1, source_target_pairs={{0,16},{8,24},{16,0},{24,8},{1,17},{9,25},{17,1},{25,9},{2,18},{10... | collective-permute-start | bytes 4325384 | tf_op jit(solution)/shard_map/ppermute | solution.py:303
  68.1 2.0 %collective-permute-start.6 = (bf16[128,2048]{1,0:T(8,128)(2,1)S(1)}, bf16[128,2048]{1,0:T(8,128)(2,1)S(1)}, u32[]{:S(2)}, u32[]{:S(2)}) collective-permute-start(bf16[128,2048]{1,0:T(8,128)(2,1)S(1)} %copy-done.3), channel_id=1, source_target_pairs={{0,8},{8,0},{16,24},{24,16},{1,9},{9,1},{17,25},{25,17},{2,10},{10... | collective-permute-start | bytes 1572872 | tf_op jit(solution)/shard_map/ppermute | solution.py:307
  68.2 2.6 %collective-permute-start.7 = (bf16[128,2048]{1,0:T(8,128)(2,1)}, bf16[128,2048]{1,0:T(8,128)(2,1)S(1)}, u32[]{:S(2)}, u32[]{:S(2)}) collective-permute-start(bf16[128,2048]{1,0:T(8,128)(2,1)} %collective-permute-done.5.refs_2_), channel_id=1, source_target_pairs={{0,8},{8,0},{16,24},{24,16},{1,9},{9,1},{17,25},{25,17},{2,10},{10... | collective-permute-start | bytes 1572872 | tf_op jit(solution)/shard_map/ppermute | solution.py:307
  73.3 3.3 %collective-permute-start.8 = (bf16[704,1024]{1,0:T(8,128)(2,1)S(1)}, bf16[704,1024]{1,0:T(8,128)(2,1)S(1)}, u32[]{:S(2)}, u32[]{:S(2)}) collective-permute-start(bf16[704,1024]{1,0:T(8,128)(2,1)S(1)} %copy-done), channel_id=1, source_target_pairs={{0,8},{8,0},{16,24},{24,16},{1,9},{9,1},{17,25},{25,17},{2,10},{10... | collective-permute-start | bytes 4325384 | tf_op jit(solution)/shard_map/ppermute | solution.py:307
  73.5 5.1 %collective-permute-start.9 = (bf16[704,1024]{1,0:T(8,128)(2,1)S(1)}, bf16[704,1024]{1,0:T(8,128)(2,1)S(1)}, u32[]{:S(2)}, u32[]{:S(2)}) collective-permute-start(bf16[704,1024]{1,0:T(8,128)(2,1)S(1)} %collective-permute-done.4.refs_2_), channel_id=1, source_target_pairs={{0,8},{8,0},{16,24},{24,16},{1,9},{9,1},{17,25},{25,17},{2,10},{10... | collective-permute-start | bytes 4325384 | tf_op jit(solution)/shard_map/ppermute | solution.py:307
  73.8 28.2 %copy-start.1 = (bf16[576,1024]{1,0:T(8,128)(2,1)S(1)}, bf16[576,1024]{1,0:T(8,128)(2,1)}, u32[]{:S(2)}) copy-start(bf16[576,1024]{1,0:T(8,128)(2,1)} %get-tuple-element.53.refs_0_) | copy-start | bytes 3538948
  73.8 28.7 %copy-start.2 = (bf16[448,1024]{1,0:T(8,128)(2,1)S(1)}, bf16[448,1024]{1,0:T(8,128)(2,1)}, u32[]{:S(2)}) copy-start(bf16[448,1024]{1,0:T(8,128)(2,1)} %get-tuple-element.56.refs_0_) | copy-start | bytes 2752516
  73.9 28.2 %collective-permute-start.3 = (bf16[576,1024]{1,0:T(8,128)(2,1)}, bf16[576,1024]{1,0:T(8,128)(2,1)S(1)}, u32[]{:S(2)}, u32[]{:S(2)}) collective-permute-start(bf16[576,1024]{1,0:T(8,128)(2,1)} %get-tuple-element.53.refs_0_), channel_id=1, source_target_pairs={{0,16},{8,24},{16,0},{24,8},{1,17},{9,25},{17,1},{25,9},{2,18},{10... | collective-permute-start | bytes 3538952 | tf_op jit(solution)/shard_map/ppermute | solution.py:303
  102.1 2.8 %collective-permute-start.10 = (bf16[576,1024]{1,0:T(8,128)(2,1)S(1)}, bf16[576,1024]{1,0:T(8,128)(2,1)S(1)}, u32[]{:S(2)}, u32[]{:S(2)}) collective-permute-start(bf16[576,1024]{1,0:T(8,128)(2,1)S(1)} %copy-done.1), channel_id=1, source_target_pairs={{0,8},{8,0},{16,24},{24,16},{1,9},{9,1},{17,25},{25,17},{2,10},{10... | collective-permute-start | bytes 3538952 | tf_op jit(solution)/shard_map/ppermute | solution.py:307
  102.1 4.5 %collective-permute-start.11 = (bf16[576,1024]{1,0:T(8,128)(2,1)S(1)}, bf16[576,1024]{1,0:T(8,128)(2,1)S(1)}, u32[]{:S(2)}, u32[]{:S(2)}) collective-permute-start(bf16[576,1024]{1,0:T(8,128)(2,1)S(1)} %collective-permute-done.3.refs_2_), channel_id=1, source_target_pairs={{0,8},{8,0},{16,24},{24,16},{1,9},{9,1},{17,25},{25,17},{2,10},{10... | collective-permute-start | bytes 3538952 | tf_op jit(solution)/shard_map/ppermute | solution.py:307
  102.6 22.8 %copy-start.4 = (bf16[192,1024]{1,0:T(8,128)(2,1)S(1)}, bf16[192,1024]{1,0:T(8,128)(2,1)}, u32[]{:S(2)}) copy-start(bf16[192,1024]{1,0:T(8,128)(2,1)} %get-tuple-element.59.refs_0_) | copy-start | bytes 1179652
  102.6 22.3 %collective-permute-start.2 = (bf16[448,1024]{1,0:T(8,128)(2,1)S(1)}, bf16[448,1024]{1,0:T(8,128)(2,1)S(1)}, u32[]{:S(2)}, u32[]{:S(2)}) collective-permute-start(bf16[448,1024]{1,0:T(8,128)(2,1)S(1)} %copy-done.2), channel_id=1, source_target_pairs={{0,16},{8,24},{16,0},{24,8},{1,17},{9,25},{17,1},{25,9},{2,18},{10... | collective-permute-start | bytes 2752520 | tf_op jit(solution)/shard_map/ppermute | solution.py:303
  124.9 2.5 %collective-permute-start.12 = (bf16[448,1024]{1,0:T(8,128)(2,1)S(1)}, bf16[448,1024]{1,0:T(8,128)(2,1)S(1)}, u32[]{:S(2)}, u32[]{:S(2)}) collective-permute-start(bf16[448,1024]{1,0:T(8,128)(2,1)S(1)} %copy-done.2), channel_id=1, source_target_pairs={{0,8},{8,0},{16,24},{24,16},{1,9},{9,1},{17,25},{25,17},{2,10},{10... | collective-permute-start | bytes 2752520 | tf_op jit(solution)/shard_map/ppermute | solution.py:307
  124.9 3.8 %collective-permute-start.13 = (bf16[448,1024]{1,0:T(8,128)(2,1)S(1)}, bf16[448,1024]{1,0:T(8,128)(2,1)S(1)}, u32[]{:S(2)}, u32[]{:S(2)}) collective-permute-start(bf16[448,1024]{1,0:T(8,128)(2,1)S(1)} %collective-permute-done.2.refs_2_), channel_id=1, source_target_pairs={{0,8},{8,0},{16,24},{24,16},{1,9},{9,1},{17,25},{25,17},{2,10},{10... | collective-permute-start | bytes 2752520 | tf_op jit(solution)/shard_map/ppermute | solution.py:307
  125.4 11.6 %copy-start.5 = (bf16[128,1024]{1,0:T(8,128)(2,1)S(1)}, bf16[128,1024]{1,0:T(8,128)(2,1)}, u32[]{:S(2)}) copy-start(bf16[128,1024]{1,0:T(8,128)(2,1)} %get-tuple-element.62.refs_0_) | copy-start | bytes 786436
  125.4 12.1 %copy-start.7 = (f32[1,1152]{1,0:T(1,128)S(1)}, f32[1,1152]{1,0:T(1,128)}, u32[]{:S(2)}) copy-start(f32[1,1152]{1,0:T(1,128)} %get-tuple-element.67) | copy-start | bytes 13828
  125.4 11.1 %collective-permute-start.1 = (bf16[192,1024]{1,0:T(8,128)(2,1)S(1)}, bf16[192,1024]{1,0:T(8,128)(2,1)S(1)}, u32[]{:S(2)}, u32[]{:S(2)}) collective-permute-start(bf16[192,1024]{1,0:T(8,128)(2,1)S(1)} %copy-done.4), channel_id=1, source_target_pairs={{0,16},{8,24},{16,0},{24,8},{1,17},{9,25},{17,1},{25,9},{2,18},{10... | collective-permute-start | bytes 1179656 | tf_op jit(solution)/shard_map/ppermute | solution.py:303
  136.5 1.7 %collective-permute-start.14 = (bf16[192,1024]{1,0:T(8,128)(2,1)S(1)}, bf16[192,1024]{1,0:T(8,128)(2,1)S(1)}, u32[]{:S(2)}, u32[]{:S(2)}) collective-permute-start(bf16[192,1024]{1,0:T(8,128)(2,1)S(1)} %copy-done.4), channel_id=1, source_target_pairs={{0,8},{8,0},{16,24},{24,16},{1,9},{9,1},{17,25},{25,17},{2,10},{10... | collective-permute-start | bytes 1179656 | tf_op jit(solution)/shard_map/ppermute | solution.py:307
  136.5 2.3 %collective-permute-start.15 = (bf16[192,1024]{1,0:T(8,128)(2,1)S(1)}, bf16[192,1024]{1,0:T(8,128)(2,1)S(1)}, u32[]{:S(2)}, u32[]{:S(2)}) collective-permute-start(bf16[192,1024]{1,0:T(8,128)(2,1)S(1)} %collective-permute-done.1.refs_2_), channel_id=1, source_target_pairs={{0,8},{8,0},{16,24},{24,16},{1,9},{9,1},{17,25},{25,17},{2,10},{10... | collective-permute-start | bytes 1179656 | tf_op jit(solution)/shard_map/ppermute | solution.py:307
  137.0 8.2 %collective-permute-start = (bf16[128,1024]{1,0:T(8,128)(2,1)S(1)}, bf16[128,1024]{1,0:T(8,128)(2,1)S(1)}, u32[]{:S(2)}, u32[]{:S(2)}) collective-permute-start(bf16[128,1024]{1,0:T(8,128)(2,1)S(1)} %copy-done.5), channel_id=1, source_target_pairs={{0,16},{8,24},{16,0},{24,8},{1,17},{9,25},{17,1},{25,9},{2,18},{10... | collective-permute-start | bytes 786440 | tf_op jit(solution)/shard_map/ppermute | solution.py:303
  138.2 8.2 %copy-start.6 = (f32[32,1,256]{2,1,0:T(1,128)S(1)}, f32[32,1,256]{2,1,0:T(1,128)}, u32[]{:S(2)}) copy-start(f32[32,1,256]{2,1,0:T(1,128)} %shard_map.160) | copy-start | bytes 98308
  145.2 1.8 %collective-permute-start.16 = (bf16[128,1024]{1,0:T(8,128)(2,1)S(1)}, bf16[128,1024]{1,0:T(8,128)(2,1)S(1)}, u32[]{:S(2)}, u32[]{:S(2)}) collective-permute-start(bf16[128,1024]{1,0:T(8,128)(2,1)S(1)} %copy-done.5), channel_id=1, source_target_pairs={{0,8},{8,0},{16,24},{24,16},{1,9},{9,1},{17,25},{25,17},{2,10},{10... | collective-permute-start | bytes 786440 | tf_op jit(solution)/shard_map/ppermute | solution.py:307
  145.3 1.9 %collective-permute-start.17 = (bf16[128,1024]{1,0:T(8,128)(2,1)S(1)}, bf16[128,1024]{1,0:T(8,128)(2,1)S(1)}, u32[]{:S(2)}, u32[]{:S(2)}) collective-permute-start(bf16[128,1024]{1,0:T(8,128)(2,1)S(1)} %collective-permute-done.refs_2_), channel_id=1, source_target_pairs={{0,8},{8,0},{16,24},{24,16},{1,9},{9,1},{17,25},{25,17},{2,10},{10... | collective-permute-start | bytes 786440 | tf_op jit(solution)/shard_map/ppermute | solution.py:307
